TPU v7x, 128 devices: a whole 4x4x4 slice. The times are simulated.
128 devices in a mesh: node: 16 (over z, y), dev: 8 (over x, core).
Axes of the slice: x: 4, y: 4, z: 4, core: 2. Of those that a mesh axis runs over, the one named last changes fastest.
Arguments:
- tokens: bfloat16 [8192, 5120], P(('node', 'dev')), may hold values from -6 to 6
- node_ids: int32 [8192, 3], P(('node', 'dev')), may hold values from 0 to 15, all different within a row; in each aligned block of 64 rows (0 to 63, 64 to 127, ...) at most 13 rows name the same one
- expert_pick: int32 [8192, 6], P(('node', 'dev')), may hold values from 0 to 8, all different within a row
- gate_share: bfloat16 [8192, 6], P(('node', 'dev')), may hold values from 0.099609375 to 1
- gate_proj: bfloat16 [48, 1536, 5120], P('node', 'dev'), may hold values from -0.078125 to 0.078125
- up_proj: bfloat16 [48, 1536, 5120], P('node', 'dev'), may hold values from -0.078125 to 0.078125
- down_proj: bfloat16 [48, 1536, 5120], P('node', 'dev'), may hold values from -0.15625 to 0.15625
Outputs:
- moe_out: bfloat16 [8192, 5120], P(('node', 'dev'))
Inputs may be any that keep to these rules, and one draw needn't show every extreme that they name: `node_ids`: A token names 3 different groups; at most 13 tokens of one device name one group, and some device reaches 13 in every draw. `expert_pick`: A token names 6 different picks; pick p selects local expert p % 3 of the token's group choice p // 3.
All inputs are finite; a program needn't handle non-finite values.
Results may differ from a plain program's by a relative error of at most 0.0085.
Values may be sent and summed in bfloat16 or wider, within the bound.
A program may use at most 256 MiB of HBM per device.

v0:
```python
import jax
import jax.numpy as jnp
from jax import lax
from jax.sharding import PartitionSpec as P


def exchange_in_groups(array, axis, split_dim, concat_dim, work, item_dim, out_dim):
    items = jax.tree.leaves(array)[0].shape[item_dim]
    count = 4 if items % 4 == 0 else 1
    finished = []
    for k in range(count):
        group = jax.tree.map(
            lambda a: lax.slice_in_dim(
                a, k * (items // count), (k + 1) * (items // count), axis=item_dim
            ),
            array,
        )
        finished.append(
            work(
                lax.all_to_all(
                    group, axis, split_axis=split_dim, concat_axis=concat_dim, tiled=True
                )
            )
        )
    return jax.tree.map(lambda *parts: jnp.concatenate(parts, axis=out_dim), *finished)


def expert_terms(tok_rows, gate_rows, gate_proj, up_proj, down_proj):
    contract = (((1,), (1,)), ((), ()))
    summed_terms = jnp.zeros((tok_rows.shape[0], down_proj.shape[2]), jnp.float32)
    for expert in range(gate_proj.shape[0]):
        gate_val = lax.dot_general(
            tok_rows, gate_proj[expert], contract, preferred_element_type=jnp.float32
        )
        up_val = lax.dot_general(
            tok_rows, up_proj[expert], contract, preferred_element_type=jnp.float32
        )
        hidden = (jax.nn.silu(gate_val) * up_val).astype(jnp.bfloat16)
        product = jnp.dot(hidden, down_proj[expert], preferred_element_type=jnp.float32)
        summed_terms = (
            summed_terms + gate_rows[:, expert : expert + 1].astype(jnp.float32) * product
        )
    return summed_terms


def shards(tokens, node_ids, expert_pick, gate_share, gate_proj, up_proj, down_proj):
    tok_count = tokens.shape[0]
    model_width = tokens.shape[1]
    node_count = lax.axis_size("node")
    dev_count = lax.axis_size("dev")
    group_choices = node_ids.shape[1]
    local_count = gate_proj.shape[0]
    slot_count = group_choices * tok_count // node_count + 1
    choose = (
        node_ids[:, :, None] == jnp.arange(node_count, dtype=jnp.int32)[None, None, :]
    ).astype(jnp.int32)
    counts = jnp.sum(choose, axis=1)
    before = jnp.cumsum(counts, axis=0) - counts
    slot_of = jnp.sum(choose * before[:, None, :], axis=2)
    placed = (slot_of[:, :, None] == jnp.arange(slot_count, dtype=jnp.int32)[None, None, :]).astype(
        jnp.float32
    )
    sel_pairs = jnp.einsum("tkn,tkc->nctk", choose.astype(jnp.float32), placed)
    selector = jnp.sum(sel_pairs, axis=3)
    picked = (
        expert_pick[:, :, None]
        == jnp.arange(group_choices * local_count, dtype=jnp.int32)[None, None, :]
    ).astype(jnp.float32)
    shares = jnp.einsum("tj,tjq->tq", gate_share.astype(jnp.float32), picked)
    shares = shares.reshape(tok_count, group_choices, local_count)
    send_rows = jnp.einsum(
        "nct,td->ncd", selector.astype(jnp.bfloat16), tokens, preferred_element_type=jnp.float32
    ).astype(jnp.bfloat16)
    send_gates = jnp.einsum("nctk,tke->nce", sel_pairs, shares).astype(jnp.bfloat16)

    def serve_group(pieces):
        got_rows, got_gates = (
            lax.all_gather(pieces[0], "dev", axis=0, tiled=True),
            lax.all_gather(pieces[1], "dev", axis=0, tiled=True),
        )
        senders, items = (got_rows.shape[0], got_rows.shape[1])
        partial_value = expert_terms(
            got_rows.reshape(senders * items, model_width),
            got_gates.reshape(senders * items, local_count),
            gate_proj,
            up_proj,
            down_proj,
        ).astype(jnp.bfloat16)
        partial_value = partial_value.reshape(senders, items, model_width)
        shares_in = lax.all_to_all(partial_value, "dev", split_axis=0, concat_axis=0, tiled=True)
        summed = jnp.sum(
            shares_in.reshape(dev_count, senders // dev_count, items, model_width),
            axis=0,
            dtype=jnp.float32,
        )
        return lax.all_to_all(summed, "node", split_axis=0, concat_axis=0, tiled=True)

    combined = exchange_in_groups((send_rows, send_gates), "node", 0, 0, serve_group, 1, 1)
    output = jnp.einsum("nct,ncd->td", selector, combined)
    return output.astype(jnp.bfloat16)


def solution(mesh):
    return jax.shard_map(
        shards,
        mesh=mesh,
        in_specs=(
            P(("node", "dev"), None),
            P(("node", "dev"), None),
            P(("node", "dev"), None),
            P(("node", "dev"), None),
            P("node", "dev", None),
            P("node", "dev", None),
            P("node", "dev", None),
        ),
        out_specs=P(("node", "dev"), None),
        check_vma=False,
    )
```

profile of v0, /device:TPU:1, one launch (start us, length us, event | category | flops | bytes accessed | tf_op | source)
XLA Modules:
  0.0 601.2 jit_solution(10169119359353929971)
XLA Ops:
  6.5 0.0 copy-start
  6.5 0.0 all-gather.2.cloned.1.call-start
  6.5 0.8 convert_reduce_fusion.1
  7.3 0.7 convert_convert_fusion
  8.0 0.1 copy.22
  8.1 0.1 reduce_window_sum.11
  8.2 0.1 copy.24
  8.2 0.7 select_reduce_fusion.1
  9.0 0.0 copy-start.3
  9.0 0.6 copy-done.3
  9.6 0.0 copy-done
  9.6 0.7 convolution_convert_fusion
  10.3 1.2 copy.28
  11.5 0.0 copy-start.5
  11.5 0.0 copy-start.6
  11.6 41.3 %all_to_all.20 = bf16[16,13,5120]{2,1,0:T(8,128)(2,1)S(1)} all-to-all(bf16[16,13,5120]{2,1,0:T(8,128)(2,1)S(1)} %copy.28), channel_id=1, replica_groups=mesh['node'=16,'dev'=8] {'node'}, dimensions={0} | all-to-all | bytes 4259840 | tf_op jit(solution)/shard_map/all_to_all | solution.py:20
  52.8 2.6 copy.29
  55.4 0.0 all-gather.2.cloned.1.call-update
  55.5 0.0 copy-done.5
  55.5 0.1 copy.25
  55.6 0.0 copy-done.6
  55.6 0.1 copy.37
  55.7 0.2 select_reduce_fusion
  55.9 0.1 copy.35
  56.0 0.3 fusion.38
  56.4 0.1 copy.26
  56.5 9.7 %all_to_all.21 = bf16[16,13,3]{1,2,0:T(4,128)(2,1)S(1)} all-to-all(bf16[16,13,3]{1,2,0:T(4,128)(2,1)S(1)} %copy.26), channel_id=1, replica_groups=mesh['node'=16,'dev'=8] {'node'}, dimensions={0} | all-to-all | bytes 2496 | tf_op jit(solution)/shard_map/all_to_all | solution.py:20
  66.2 16.3 %all_gather.6 = bf16[128,13,3]{1,0,2:T(8,128)(2,1)S(1)} all-gather(bf16[16,13,3]{1,0,2:T(8,128)(2,1)S(1)} %copy.27), channel_id=1, replica_groups=mesh['node'=16,'dev'=8] {'dev'}, dimensions={0}, use_global_device_ids=true | all-gather | bytes 11232 | tf_op jit(solution)/shard_map/all_gather | solution.py:79
  82.5 0.2 reshape.28
  82.7 0.1 fusion.52
  82.8 58.5 %all-gather.2.cloned.1.call-done = bf16[128,13,5120]{2,0,1:T(8,128)(2,1)} async-done(((bf16[16,13,5120]{2,0,1:T(8,128)(2,1)}), bf16[128,13,5120]{2,0,1:T(8,128)(2,1)}) %all-gather.2.cloned.1.call-update) | async-done | bytes 17039376 | tf_op jit(solution)/shard_map/all_gather | solution.py:78
  141.3 21.0 %copy.30 = bf16[128,13,5120]{2,1,0:T(8,128)(2,1)} copy(bf16[128,13,5120]{2,0,1:T(8,128)(2,1)} %all-gather.2.cloned.1.call-done) | data formatting | bytes 34078720 | tf_op jit(solution)/shard_map/all_gather | solution.py:78
  162.3 20.7 %reshape.29 = bf16[1664,5120]{1,0:T(8,128)(2,1)} reshape(bf16[128,13,5120]{2,1,0:T(8,128)(2,1)} %copy.30) | data formatting | bytes 34078720 | tf_op jit(solution)/shard_map/reshape | solution.py:83
  183.0 0.0 copy-start.2
  183.0 12.3 %fusion.7 = f32[1664,192]{0,1:T(8,128)S(1)} fusion(bf16[1664,5120]{1,0:T(8,128)(2,1)} %reshape.29, bf16[3,192,5120]{2,1,0:T(8,128)(2,1)} %param.11), kind=kOutput, calls=%fused_computation.14 | convolution fusion | flops 3271557120 | bytes 20283392 | tf_op jit(solution)/shard_map/dot_general | solution.py:32
  195.3 0.0 copy-done.2
  195.3 7.2 %fusion.12 = f32[1664,192]{0,1:T(8,128)S(1)} fusion(bf16[1664,5120]{1,0:T(8,128)(2,1)S(1)} %copy-done.2, bf16[3,192,5120]{2,1,0:T(8,128)(2,1)} %param.11), kind=kOutput, calls=%fused_computation.19 | convolution fusion | flops 3271557120 | bytes 20283392 | tf_op jit(solution)/shard_map/dot_general | solution.py:32
  202.5 7.2 %fusion.17 = f32[1664,192]{0,1:T(8,128)S(1)} fusion(bf16[1664,5120]{1,0:T(8,128)(2,1)S(1)} %copy-done.2, bf16[3,192,5120]{2,1,0:T(8,128)(2,1)} %param.11), kind=kOutput, calls=%fused_computation.24 | convolution fusion | flops 3271557120 | bytes 20283392 | tf_op jit(solution)/shard_map/dot_general | solution.py:32
  209.7 7.4 %fusion.4.clone.5 = bf16[1664,192]{0,1:T(8,128)(2,1)S(1)} fusion(bf16[1664,5120]{1,0:T(8,128)(2,1)S(1)} %copy-done.2, bf16[3,192,5120]{2,1,0:T(8,128)(2,1)} %param.12, f32[1664,192]{0,1:T(8,128)S(1)} %fusion.7), kind=kOutput, calls=%fused_computation.11.clone.clone.clone.2 | convolution fusion | flops 3273474048 | bytes 20922368 | tf_op jit(solution)/shard_map/dot_general | solution.py:35
  217.2 23.2 %fusion.14 = f32[1664,5120]{1,0:T(8,128)} fusion(bf16[3,192,5120]{2,1,0:T(8,128)(2,1)} %param.13, bf16[1664,5120]{1,0:T(8,128)(2,1)} %reshape.29, bf16[3,192,5120]{2,1,0:T(8,128)(2,1)} %param.12, f32[1664,192]{0,1:T(8,128)S(1)} %fusion.17), kind=kOutput, calls=%fused_computation.21 | convolution fusion | flops 6545031168 | bytes 56328192 | tf_op jit(solution)/shard_map/dot_general | solution.py:39
  240.4 23.2 %fusion.9 = f32[1664,5120]{1,0:T(8,128)} fusion(bf16[3,192,5120]{2,1,0:T(8,128)(2,1)} %param.13, bf16[1664,5120]{1,0:T(8,128)(2,1)} %reshape.29, bf16[3,192,5120]{2,1,0:T(8,128)(2,1)} %param.12, f32[1664,192]{0,1:T(8,128)S(1)} %fusion.12), kind=kOutput, calls=%fused_computation.16 | convolution fusion | flops 6545031168 | bytes 56328192 | tf_op jit(solution)/shard_map/dot_general | solution.py:39
  263.6 30.3 %add_convert_fusion = bf16[1664,5120]{1,0:T(8,128)(2,1)} fusion(f32[1664,5120]{1,0:T(8,128)} %fusion.9, f32[1664,5120]{1,0:T(8,128)} %fusion.14, f32[1664]{0:T(1024)S(1)} %get-tuple-element.6, f32[1664]{0:T(1024)S(1)} %get-tuple-element.7, f32[1664]{0:T(1024)S(1)} %get-tuple-element.5, bf16[3,192,5120]{2,1,0:T(8,128)(2,1)} %param.13, ...), kind=kOutput, calls=%fused_computation.1 | convolution fusion | flops 3322675200 | bytes 87821824 | tf_op jit(solution)/shard_map/dot_general | solution.py:39
  293.9 20.2 %reshape.30 = bf16[128,13,5120]{2,1,0:T(8,128)(2,1)} reshape(bf16[1664,5120]{1,0:T(8,128)(2,1)} %add_convert_fusion) | data formatting | bytes 34078720 | tf_op jit(solution)/shard_map/reshape | solution.py:89
  314.1 233.2 %all_to_all.22 = bf16[128,13,5120]{2,1,0:T(8,128)(2,1)S(1)} all-to-all(bf16[128,13,5120]{2,1,0:T(8,128)(2,1)} %reshape.30), channel_id=1, replica_groups=mesh['node'=16,'dev'=8] {'dev'}, dimensions={0} | all-to-all | bytes 34078720 | tf_op jit(solution)/shard_map/all_to_all | solution.py:90
  547.3 4.8 convert_reduce_fusion
  552.1 39.5 %all_to_all.23 = bf16[16,13,5120]{2,1,0:T(8,128)(2,1)S(1)} all-to-all(bf16[16,13,5120]{2,1,0:T(8,128)(2,1)S(1)} %convert_reduce_fusion), channel_id=1, replica_groups=mesh['node'=16,'dev'=8] {'node'}, dimensions={0} | all-to-all | bytes 4259840 | tf_op jit(solution)/shard_map/all_to_all | solution.py:96
  591.6 0.0 copy-done.4
  591.6 2.3 fusion
  (8 shorter events, 0.1 us)
Async XLA Ops:
  6.5 3.1 copy-start
  6.5 134.8 %all-gather.2.cloned.1.call-start = ((), (), s32[]{:S(2)}) async-start(), calls=%async_computation.4 | async-start | bytes 19169280 | tf_op jit(solution)/shard_map/all_gather | solution.py:78
  9.0 0.6 copy-start.3
  11.5 43.9 %copy-start.5 = (s32[64,6]{0,1:T(8,128)S(1)}, s32[64,6]{0,1:T(8,128)}, u32[]{:S(2)}) copy-start(s32[64,6]{0,1:T(8,128)} %param.9) | copy-start | bytes 4612
  11.5 44.0 %copy-start.6 = (bf16[64,6]{0,1:T(8,128)(2,1)S(1)}, bf16[64,6]{0,1:T(8,128)(2,1)}, u32[]{:S(2)}) copy-start(bf16[64,6]{0,1:T(8,128)(2,1)} %param.10) | copy-start | bytes 2308
  183.0 12.3 %copy-start.2 = (bf16[1664,5120]{1,0:T(8,128)(2,1)S(1)}, bf16[1664,5120]{1,0:T(8,128)(2,1)}, u32[]{:S(2)}) copy-start(bf16[1664,5120]{1,0:T(8,128)(2,1)} %reshape.29) | copy-start | bytes 51118084
  547.3 44.3 %copy-start.4 = (bf16[16,13,64]{2,0,1:T(8,128)(2,1)S(1)}, bf16[16,13,64]{2,0,1:T(8,128)(2,1)}, u32[]{:S(2)}) copy-start(bf16[16,13,64]{2,0,1:T(8,128)(2,1)} %copy-done.3) | copy-start | bytes 79876
  547.3 46.6 %copy-start.1 = (bf16[64,5120]{1,0:T(8,128)(2,1)S(1)}, bf16[64,5120]{1,0:T(8,128)(2,1)}, u32[]{:S(2)}) copy-start(bf16[64,5120]{1,0:T(8,128)(2,1)} %param.7) | copy-start | bytes 1966084
Sparse Core Ops, SparseCore 0:
  55.6 85.6 all-gather.1
where the time goes:
time: 611 us; the launch traced here: 601 us
  blocking collectives  340 us (56%)
  matrix products  114 us (19%)
  local copies, waits for them, and re-layouts  67.1 us (11%)
  waiting for transfers between devices  58.5 us (10%)
  between operations  14 us (2%)
  other arithmetic  7.36 us (1%)
    all_to_all x1, blocking collectives, serve_group(): lax.all_to_all(partial_value, 'dev', split_axis=0, concat_axis=0, tiled=T...  233 us
    dot_general x3, matrix products, expert_terms(): jnp.dot(hidden, down_proj[expert], preferred_element_type=jnp.float32)  76.7 us
    all_gather x1, waiting for transfers between devices, serve_group(): lax.all_gather(pieces[0], 'dev', axis=0, tiled=True)  58.5 us
    all_to_all x2, blocking collectives, exchange_in_groups(): lax.all_to_all(group, axis, split_axis=split_dim, concat_axis=concat_dim,...  51 us
    all_to_all x1, blocking collectives, serve_group(): lax.all_to_all(summed, 'node', split_axis=0, concat_axis=0, tiled=True)  39.5 us
    dot_general x3, matrix products, expert_terms(): lax.dot_general(tok_rows, gate_proj[expert], contract, preferred_element_...  26.7 us
    all_gather x1, local copies, waits for them, and re-layouts, serve_group(): lax.all_gather(pieces[0], 'dev', axis=0, tiled=True)  21 us
    reshape x1, local copies, waits for them, and re-layouts, serve_group(): got_rows.reshape(senders * items, model_width)  20.7 us
  transfers between devices with their start and end apart: 1, of which 1 were waited for; matrix products, arithmetic and copies ran while one was open for 0% of the time, Pallas kernels for 0%

commit v1 on v0

v1 whole, which is shorter than its diff:
```python
import functools

import jax
import jax.numpy as jnp
from jax import lax
from jax.experimental import pallas as pl
from jax.experimental.pallas import tpu as pltpu
from jax.sharding import PartitionSpec as P

MESH = pl.DeviceIdType.MESH
BF = jnp.bfloat16
F32 = jnp.float32

CAP = 13
PAD = 16
OFFS = (
    (0, 0), (0, 1), (1, 0), (3, 3),
    (3, 1), (0, 2), (2, 0), (1, 2), (2, 1), (3, 2), (2, 3), (2, 2),
    (1, 3), (1, 1), (3, 0), (0, 3),
)
N_OFF = len(OFFS)
ROWS = N_OFF * CAP
TILES = (3, 4, 3, 3)
OWN, LEFT, RIGHT, OPP = 0, 1, 2, 3


def kernel(
    tok_ref, ids_ref, pick_ref, share_ref, wg_hbm, wu_hbm, wd_hbm, out_ref,
    wg, wu, wd, xbuf, prbuf, rabuf, rbbuf, flbuf, frbuf, send, land, ret, hid, gp, sel,
    w_sem, ds_sem, dr_sem, gs_sem, gr_sem, as_sem, ar_sem, rs_sem, rr_sem, bs_sem, br_sem,
):
    toks, width = tok_ref.shape
    half = width // 2
    experts, units = wg.shape[0], wg.shape[1]
    chunks = len(TILES)
    bounds = [0]
    for t in TILES:
        bounds.append(bounds[-1] + t * PAD)
    step = min(512, half)
    slots_all = N_OFF * PAD

    me_n = lax.axis_index("node")
    me_d = lax.axis_index("dev")
    z, y = me_n // 4, me_n % 4
    x, c = me_d // 2, me_d % 2

    def node_at(dz, dy):
        return ((z + dz) % 4) * 4 + (y + dy) % 4

    def dev_at(dx, dc):
        return ((x + dx) % 4) * 2 + (c + dc) % 2

    to_right, to_left, to_core = dev_at(1, 0), dev_at(3, 0), dev_at(0, 1)

    loads = []
    for i, (src, dst) in enumerate(((wg_hbm, wg), (wu_hbm, wu), (wd_hbm, wd))):
        load = pltpu.make_async_copy(src, dst, w_sem.at[i])
        load.start()
        loads.append(load)

    barrier = pltpu.get_barrier_semaphore()
    peers = [(node_at(dz, dy), me_d) for dz, dy in OFFS[1:]]
    peers += [(me_n, dev_at(dx, dc)) for dx in range(4) for dc in range(2) if (dx, dc) != (0, 0)]
    for peer in peers:
        pl.semaphore_signal(barrier, inc=1, device_id=peer, device_id_type=MESH)

    def remote(src, dst, s_sem, r_sem, device):
        return pltpu.make_async_remote_copy(
            src_ref=src, dst_ref=dst, send_sem=s_sem, recv_sem=r_sem,
            device_id=device, device_id_type=MESH,
        )

    col = lax.broadcasted_iota(jnp.int32, (toks, slots_all), 1)
    block, slot = col // PAD, col % PAD
    dest = jnp.zeros((toks, slots_all), jnp.int32)
    for r, (dz, dy) in enumerate(OFFS):
        dest = jnp.where(block == r, node_at(dz, dy), dest)
    ids = ids_ref[...]
    choice = [(ids[:, k : k + 1] == dest).astype(F32) for k in range(ids.shape[1])]
    chosen = choice[0] + choice[1] + choice[2]
    earlier = (
        lax.broadcasted_iota(jnp.int32, (toks, toks), 0)
        > lax.broadcasted_iota(jnp.int32, (toks, toks), 1)
    ).astype(BF)
    rank = jnp.dot(earlier, chosen.astype(BF), preferred_element_type=F32)
    picked = jnp.where(rank == slot.astype(F32), chosen, 0.0)
    sel[...] = picked.astype(BF)
    sel_t = picked.T.astype(BF)
    pick, share = pick_ref[...], share_ref[...].astype(F32)
    gates = jnp.zeros((slots_all, 128), F32)
    lane = lax.broadcasted_iota(jnp.int32, (toks, 128), 1)
    for e in range(experts):
        weight = jnp.zeros((toks, slots_all), F32)
        for k in range(len(choice)):
            part = jnp.sum(jnp.where(pick == k * experts + e, share, 0.0), axis=1, keepdims=True)
            weight = weight + choice[k] * part
        weight_t = (weight * picked).T.astype(BF)
        gates = gates + jnp.dot(weight_t, (lane == e).astype(BF), preferred_element_type=F32)
    send[:, :, width:] = gates.astype(BF).reshape(N_OFF, PAD, 128)

    def fill_send(i, carry):
        cols = pl.ds(pl.multiple_of(i * step, step), step)
        rows = jnp.dot(sel_t, tok_ref[:, cols], preferred_element_type=F32)
        send[:, :, cols] = rows.astype(BF).reshape(N_OFF, PAD, step)
        return carry

    lax.fori_loop(0, width // step, fill_send, 0)

    pl.semaphore_wait(barrier, len(peers))
    dispatch = [None]
    for r in range(1, N_OFF):
        copy = remote(
            send.at[r], land.at[r], ds_sem.at[r], dr_sem.at[r], (node_at(*OFFS[r]), me_d)
        )
        copy.start()
        dispatch.append(copy)
    land[0] = send[0]

    def rows_of(k):
        return pl.ds(bounds[k], bounds[k + 1] - bounds[k])

    low, high = pl.ds(0, half), pl.ds(half, half)
    all_cols = pl.ds(0, width)

    def gather_copy(k, j, src, dst, cols, device):
        return remote(
            xbuf.at[src, rows_of(k), cols], xbuf.at[dst, rows_of(k), cols],
            as_sem.at[k, j], ar_sem.at[k, j], (me_n, device),
        )

    gather = [
        (
            gather_copy(k, 0, OWN, LEFT, all_cols, to_right),
            gather_copy(k, 1, OWN, RIGHT, all_cols, to_left),
            gather_copy(k, 2, LEFT, OPP, low, to_right),
            gather_copy(k, 3, RIGHT, OPP, high, to_left),
            gather_copy(k, 4, OWN, 4 + OWN, all_cols, to_core),
            gather_copy(k, 5, LEFT, 4 + LEFT, all_cols, to_core),
            gather_copy(k, 6, RIGHT, 4 + RIGHT, all_cols, to_core),
            gather_copy(k, 7, OPP, 4 + OPP, all_cols, to_core),
        )
        for k in range(chunks)
    ]

    def spread(rows, row0, slots, slot0):
        at = lax.broadcasted_iota(jnp.int32, (rows, slots), 0) + row0
        frm = lax.broadcasted_iota(jnp.int32, (rows, slots), 1) + slot0
        same = at == CAP * (frm // PAD) + frm % PAD
        return (same & (frm % PAD < CAP)).astype(BF)

    arrived = [0]

    def deliver(k):
        lo, hi = bounds[k], bounds[k + 1]
        first, last = lo // CAP, min(N_OFF, (hi - 1) // CAP + 1)
        while arrived[0] < last - 1:
            arrived[0] += 1
            dispatch[arrived[0]].wait_recv()
        pack = spread(hi - lo, lo, (last - first) * PAD, first * PAD)

        def body(i, carry):
            cols = pl.ds(pl.multiple_of(i * step, step), step)
            got = land[first:last, :, cols].reshape((last - first) * PAD, step)
            xbuf[OWN, lo:hi, cols] = jnp.dot(pack, got, preferred_element_type=F32).astype(BF)
            return carry

        lax.fori_loop(0, width // step, body, 0)
        for j in (0, 1, 4):
            gather[k][j].start()

    def relay(k):
        gather[k][0].wait_recv()
        gather[k][2].start()
        gather[k][5].start()
        gather[k][1].wait_recv()
        gather[k][3].start()
        gather[k][6].start()

    def relay_opp(k):
        gather[k][2].wait_recv()
        gather[k][3].wait_recv()
        gather[k][7].start()

    gate_copies = []

    def share_gates():
        pack = spread(ROWS, 0, slots_all, 0)
        got = land[:, :, width:].reshape(slots_all, 128)
        flat = jnp.dot(pack, got, preferred_element_type=F32).astype(BF)
        packed = jnp.zeros((PAD, 128), F32)
        e_at = lax.broadcasted_iota(jnp.int32, (128, 128), 0)
        l_at = lax.broadcasted_iota(jnp.int32, (128, 128), 1)
        for t in range(ROWS // PAD):
            move = ((e_at < experts) & (l_at == experts * t + e_at)).astype(BF)
            packed = packed + jnp.dot(
                flat[t * PAD : (t + 1) * PAD], move, preferred_element_type=F32
            )
        gp[0] = packed.astype(BF)
        n = 0
        for dx, there in ((0, OWN), (1, LEFT), (3, RIGHT), (2, OPP)):
            for dc in (0, 1):
                if (dx, dc) == (0, 0):
                    continue
                copy = remote(
                    gp.at[0], gp.at[4 * dc + there], gs_sem.at[n], gr_sem.at[n],
                    (me_n, dev_at(dx, dc)),
                )
                copy.start()
                gate_copies.append(copy)
                n += 1

    def hidden(k):
        lo, hi = bounds[k], bounds[k + 1]
        m = 8 * (hi - lo)
        for j in (4, 5, 6, 7):
            gather[k][j].wait_recv()
        contract = (((1,), (1,)), ((), ()))
        columns = []
        for e in range(experts):
            pieces = []
            for s in range(8):
                for t in range(lo // PAD, hi // PAD):
                    at = experts * t + e
                    pieces.append(gp[s, :, at : at + 1].astype(F32))
            columns.append(jnp.concatenate(pieces, axis=0))
        for e in range(experts):
            rows = xbuf[:, lo:hi, :].reshape(m, width)
            gate_val = lax.dot_general(rows, wg[e], contract, preferred_element_type=F32)
            up_val = lax.dot_general(rows, wu[e], contract, preferred_element_type=F32)
            act = gate_val / (1.0 + jnp.exp(-gate_val)) * up_val
            hid[e, 0:m, :] = (act * columns[e]).astype(BF)

    def reduce_copy(k, j, src, dst, cols, device, n=None):
        return remote(
            src.at[rows_of(k), cols], dst.at[rows_of(k), cols],
            rs_sem.at[k, j], rr_sem.at[k, j], (me_n, device),
        )

    reduce = [
        (
            remote(
                xbuf.at[4:8, rows_of(k), low], prbuf.at[:, rows_of(k), low],
                rs_sem.at[k, 0], rr_sem.at[k, 0], (me_n, to_core),
            ),
            remote(
                xbuf.at[4:8, rows_of(k), high], prbuf.at[:, rows_of(k), high],
                rs_sem.at[k, 1], rr_sem.at[k, 1], (me_n, to_core),
            ),
            reduce_copy(k, 2, xbuf.at[OPP, :, low], rabuf, low, to_right),
            reduce_copy(k, 3, xbuf.at[OPP, :, high], rbbuf, low, to_left),
            reduce_copy(k, 4, xbuf.at[RIGHT], flbuf, high, to_right),
            reduce_copy(k, 5, xbuf.at[LEFT], frbuf, low, to_left),
            reduce_copy(k, 6, xbuf.at[RIGHT], flbuf, low, to_right),
            reduce_copy(k, 7, xbuf.at[LEFT], frbuf, high, to_left),
        )
        for k in range(chunks)
    ]

    def project(k):
        lo, hi = bounds[k], bounds[k + 1]
        m = 8 * (hi - lo)
        for j in range(8):
            gather[k][j].wait_send()

        def body(i, carry):
            cols = pl.ds(pl.multiple_of(i * step, step), step)
            total = jnp.dot(hid[0, 0:m, :], wd[0, :, cols], preferred_element_type=F32)
            for e in range(1, experts):
                total += jnp.dot(hid[e, 0:m, :], wd[e, :, cols], preferred_element_type=F32)
            xbuf[:, lo:hi, cols] = total.astype(BF).reshape(8, hi - lo, step)
            return carry

        lax.fori_loop(0, half // step, body, 0)
        reduce[k][0].start()
        lax.fori_loop(half // step, width // step, body, 0)
        reduce[k][1].start()

    def add_up(k, place, start, others):
        lo, hi = bounds[k], bounds[k + 1]

        def body(i, carry):
            at = pl.multiple_of(i * step, step)
            cols = pl.ds(start + at, step)
            total = xbuf[place, lo:hi, cols].astype(F32)
            for other, shift in others:
                total += other[lo:hi, pl.ds(at + shift, step)].astype(F32)
            xbuf[place, lo:hi, cols] = total.astype(BF)
            return carry

        lax.fori_loop(0, half // step, body, 0)

    def pass_on(k):
        reduce[k][0].wait_recv()
        add_up(k, OPP, 0, ((prbuf.at[OPP], 0),))
        reduce[k][2].start()
        reduce[k][1].wait_recv()
        add_up(k, OPP, half, ((prbuf.at[OPP], half),))
        reduce[k][3].start()
        add_up(k, RIGHT, half, ((prbuf.at[RIGHT], half),))
        reduce[k][4].start()
        add_up(k, LEFT, 0, ((prbuf.at[LEFT], 0),))
        reduce[k][5].start()

    def pass_home(k):
        reduce[k][2].wait_recv()
        add_up(k, RIGHT, 0, ((prbuf.at[RIGHT], 0), (rabuf, 0)))
        reduce[k][6].start()
        reduce[k][3].wait_recv()
        add_up(k, LEFT, half, ((prbuf.at[LEFT], half), (rbbuf, 0)))
        reduce[k][7].start()

    returns = [None]
    returned = [0]

    def give_back(k):
        lo, hi = bounds[k], bounds[k + 1]
        for j in (4, 5, 6, 7):
            reduce[k][j].wait_recv()
        for start in (0, half):
            add_up(k, OWN, start, ((prbuf.at[OWN], start), (flbuf, start), (frbuf, start)))
        first, last = returned[0], hi // CAP
        returned[0] = last
        row0 = first * CAP // PAD * PAD
        unpack = (
            lax.broadcasted_iota(jnp.int32, ((last - first) * PAD, hi - row0), 1) + row0
        )
        frm = lax.broadcasted_iota(jnp.int32, ((last - first) * PAD, hi - row0), 0) + first * PAD
        unpack = ((unpack == CAP * (frm // PAD) + frm % PAD) & (frm % PAD < CAP)).astype(BF)
        own = 1 if first == 0 else 0

        def body(i, carry):
            cols = pl.ds(pl.multiple_of(i * step, step), step)
            back = jnp.dot(unpack, xbuf[OWN, row0:hi, cols], preferred_element_type=F32)
            back = back.astype(BF).reshape(last - first, PAD, step)
            if own:
                ret[0, :, cols] = back[0]
            send[first + own : last, :, cols] = back[own:]
            return carry

        lax.fori_loop(0, width // step, body, 0)
        for r in range(first + own, last):
            dz, dy = OFFS[r]
            copy = remote(
                send.at[r, :, all_cols], ret.at[r], bs_sem.at[r], br_sem.at[r],
                (node_at(-dz, -dy), me_d),
            )
            copy.start()
            returns.append(copy)

    deliver(0)
    deliver(1)
    relay(0)
    deliver(2)
    relay(1)
    relay_opp(0)
    deliver(3)
    share_gates()
    relay(2)
    relay_opp(1)
    for load in loads:
        load.wait()
    for copy in gate_copies:
        copy.wait_recv()
    hidden(0)
    project(0)
    relay(3)
    relay_opp(2)
    hidden(1)
    pass_on(0)
    project(1)
    relay_opp(3)
    pass_home(0)
    hidden(2)
    pass_on(1)
    project(2)
    pass_home(1)
    hidden(3)
    pass_on(2)
    project(3)
    for r in range(1, N_OFF):
        dispatch[r].wait_send()
    pass_on(3)
    give_back(0)
    pass_home(2)
    give_back(1)
    pass_home(3)
    give_back(2)
    give_back(3)

    for r in range(1, N_OFF):
        returns[r].wait_recv()

    def combine(i, carry):
        cols = pl.ds(pl.multiple_of(i * step, step), step)
        got = ret[:, :, cols].reshape(slots_all, step)
        out_ref[:, cols] = jnp.dot(sel[...], got, preferred_element_type=F32).astype(BF)
        return carry

    lax.fori_loop(0, width // step, combine, 0)

    for copy in gate_copies:
        copy.wait_send()
    for k in range(chunks):
        for copy in reduce[k]:
            copy.wait_send()
    for r in range(1, N_OFF):
        returns[r].wait_send()


def shards(tokens, node_ids, expert_pick, gate_share, gate_proj, up_proj, down_proj):
    toks, width = tokens.shape
    experts, units, _ = gate_proj.shape
    half = width // 2
    chunks = len(TILES)
    vmem = pl.BlockSpec(memory_space=pltpu.VMEM)
    hbm = pl.BlockSpec(memory_space=pl.ANY)
    dma = pltpu.SemaphoreType.DMA
    weights = pltpu.VMEM((experts, units, width), BF)
    return pl.pallas_call(
        kernel,
        out_shape=jax.ShapeDtypeStruct((toks, width), BF),
        in_specs=[vmem] * 4 + [hbm] * 3,
        out_specs=vmem,
        scratch_shapes=[
            weights,
            weights,
            weights,
            pltpu.VMEM((8, ROWS, width), BF),
            pltpu.VMEM((4, ROWS, width), BF),
            pltpu.VMEM((ROWS, half), BF),
            pltpu.VMEM((ROWS, half), BF),
            pltpu.VMEM((ROWS, width), BF),
            pltpu.VMEM((ROWS, width), BF),
            pltpu.VMEM((N_OFF, PAD, width + 128), BF),
            pltpu.VMEM((N_OFF, PAD, width + 128), BF),
            pltpu.VMEM((N_OFF, PAD, width), BF),
            pltpu.VMEM((experts, 8 * PAD * max(TILES), units), BF),
            pltpu.VMEM((8, PAD, 128), BF),
            pltpu.VMEM((toks, N_OFF * PAD), BF),
            dma((3,)),
            dma((N_OFF,)),
            dma((N_OFF,)),
            dma((7,)),
            dma((7,)),
            dma((chunks, 8)),
            dma((chunks, 8)),
            dma((chunks, 8)),
            dma((chunks, 8)),
            dma((N_OFF,)),
            dma((N_OFF,)),
        ],
        compiler_params=pltpu.CompilerParams(
            collective_id=0, has_side_effects=True, vmem_limit_bytes=67043328
        ),
    )(tokens, node_ids, expert_pick, gate_share, gate_proj, up_proj, down_proj)


def solution(mesh):
    return jax.shard_map(
        shards,
        mesh=mesh,
        in_specs=(
            P(("node", "dev"), None),
            P(("node", "dev"), None),
            P(("node", "dev"), None),
            P(("node", "dev"), None),
            P("node", "dev", None),
            P("node", "dev", None),
            P("node", "dev", None),
        ),
        out_specs=P(("node", "dev"), None),
        check_vma=False,
    )
```

time: 611 us -> 207 us (0.34); the launches traced: 601 us -> 207 us
  blocking collectives: 340 us -> 0 us
  Pallas kernels: 0 us -> 201 us
  matrix products: 114 us -> 0 us
  local copies, waits for them, and re-layouts: 67.1 us -> 6.1 us
  waiting for transfers between devices: 58.5 us -> 0 us
  between operations: 14 us -> 0.01 us
  other arithmetic: 7.36 us -> 0 us
    all_to_all x4 -> x0, blocking collectives: 324 us -> none  [the longest x1 233 us: serve_group(): lax.all_to_all(partial_value, 'dev', split_axis=0, concat_axis=0, tiled=T...]
    pallas_call x0 -> x1, Pallas kernels: none -> 201 us  [shards(): pl.pallas_call(kernel, out_shape=jax.ShapeDtypeStruct((toks, width), BF),...]
    dot_general x10 -> x0, matrix products: 114 us -> none  [the longest x3 76.7 us: expert_terms(): jnp.dot(hidden, down_proj[expert], preferred_element_type=jnp.float32)]
    all_gather x1 -> x0, waiting for transfers between devices: 58.5 us -> none  [serve_group(): lax.all_gather(pieces[0], 'dev', axis=0, tiled=True)]
    reshape x4 -> x0, local copies, waits for them, and re-layouts: 41.1 us -> none  [the longest x1 20.7 us: serve_group(): got_rows.reshape(senders * items, model_width)]
    all_gather x1 -> x0, local copies, waits for them, and re-layouts: 21 us -> none  [serve_group(): lax.all_gather(pieces[0], 'dev', axis=0, tiled=True)]
    all_gather x1 -> x0, blocking collectives: 16.3 us -> none  [serve_group(): lax.all_gather(pieces[1], 'dev', axis=0, tiled=True)]
    reduce_sum x4 -> x0, other arithmetic: 6.28 us -> none  [the longest x1 4.77 us: serve_group(): jnp.sum(shares_in.reshape(dev_count, senders // dev_count, items, model_w...]
  transfers between devices with their start and end apart: 1 -> 0, of which waited for: 1 -> 0; matrix products, arithmetic and copies ran while one was open for 0% -> 0% of each run, Pallas kernels for 0% -> 0%
where the time goes in v1:
time: 207 us
  Pallas kernels  201 us (97%)
  local copies, waits for them, and re-layouts  6.1 us (3%)
    pallas_call x1, Pallas kernels, shards(): pl.pallas_call(kernel, out_shape=jax.ShapeDtypeStruct((toks, width), BF),...  201 us
    unnamed x4, local copies, waits for them, and re-layouts  6.1 us

profile of v1, /device:TPU:1, one launch (start us, length us, event | category | flops | bytes accessed | tf_op | source)
XLA Modules:
  0.0 206.7 jit_solution(2231724530494064660)
XLA Ops:
  0.0 1.4 copy.10.share_ref
  1.4 1.4 copy.8.ids_ref
  2.8 1.4 copy.9.pick_ref
  4.1 200.6 %shard_map.73 = bf16[64,5120]{1,0:T(8,128)(2,1)} custom-call(bf16[64,5120]{1,0:T(8,128)(2,1)} %tok_ref.1, s32[64,3]{1,0:T(8,128)} %copy.8.ids_ref, s32[64,6]{1,0:T(8,128)} %copy.9.pick_ref, bf16[64,6]{1,0:T(8,128)(2,1)} %copy.10.share_ref, bf16[3,192,5120]{2,1,0:T(8,128)(2,1)} %wg_hbm.1, bf16[3,192,5120]{2,1,0:T(8,128)(2,1)} %wu_hbm.1, ...), custom_call_target="tpu_custom_call" | custom-call | tf_op jit(solution)/shard_map/pallas_call | solution.py:419
  204.7 2.0 copy.12

commit v2 on v1

--- a/solution.py
+++ b/solution.py
@@ -15,19 +15,21 @@
 PAD = 16
 OFFS = (
     (0, 0), (0, 1), (1, 0), (3, 3),
-    (3, 1), (0, 2), (2, 0), (1, 2), (2, 1), (3, 2), (2, 3), (2, 2),
-    (1, 3), (1, 1), (3, 0), (0, 3),
+    (2, 2), (1, 2), (2, 1), (0, 2), (2, 0),
+    (3, 2), (2, 3), (3, 1), (1, 3),
+    (1, 1), (3, 0), (0, 3),
 )
 N_OFF = len(OFFS)
+WAVES = (1, 4, 9, N_OFF)
 ROWS = N_OFF * CAP
-TILES = (3, 4, 3, 3)
+TILES = (3, 4, 4, 2)
 OWN, LEFT, RIGHT, OPP = 0, 1, 2, 3
 
 
 def kernel(
     tok_ref, ids_ref, pick_ref, share_ref, wg_hbm, wu_hbm, wd_hbm, out_ref,
-    wg, wu, wd, xbuf, prbuf, rabuf, rbbuf, flbuf, frbuf, send, land, ret, hid, gp, sel,
-    w_sem, ds_sem, dr_sem, gs_sem, gr_sem, as_sem, ar_sem, rs_sem, rr_sem, bs_sem, br_sem,
+    wg, wu, wd, xbuf, prbuf, rabuf, rbbuf, flbuf, frbuf, send, land, ret, hid, gp, sel, total,
+    o_sem, w_sem, ds_sem, dr_sem, gs_sem, gr_sem, as_sem, ar_sem, rs_sem, rr_sem, bs_sem, br_sem,
 ):
     toks, width = tok_ref.shape
     half = width // 2
@@ -70,32 +72,31 @@
             device_id=device, device_id_type=MESH,
         )
 
-    col = lax.broadcasted_iota(jnp.int32, (toks, slots_all), 1)
-    block, slot = col // PAD, col % PAD
-    dest = jnp.zeros((toks, slots_all), jnp.int32)
+    row = lax.broadcasted_iota(jnp.int32, (slots_all, toks), 0)
+    block, slot = row // PAD, row % PAD
+    dest = jnp.zeros((slots_all, toks), jnp.int32)
     for r, (dz, dy) in enumerate(OFFS):
         dest = jnp.where(block == r, node_at(dz, dy), dest)
     ids = ids_ref[...]
-    choice = [(ids[:, k : k + 1] == dest).astype(F32) for k in range(ids.shape[1])]
+    choice = [(ids[k : k + 1, :] == dest).astype(F32) for k in range(ids.shape[0])]
     chosen = choice[0] + choice[1] + choice[2]
     earlier = (
         lax.broadcasted_iota(jnp.int32, (toks, toks), 0)
-        > lax.broadcasted_iota(jnp.int32, (toks, toks), 1)
+        < lax.broadcasted_iota(jnp.int32, (toks, toks), 1)
     ).astype(BF)
-    rank = jnp.dot(earlier, chosen.astype(BF), preferred_element_type=F32)
+    rank = jnp.dot(chosen.astype(BF), earlier, preferred_element_type=F32)
     picked = jnp.where(rank == slot.astype(F32), chosen, 0.0)
-    sel[...] = picked.astype(BF)
-    sel_t = picked.T.astype(BF)
+    sel_t = picked.astype(BF)
     pick, share = pick_ref[...], share_ref[...].astype(F32)
     gates = jnp.zeros((slots_all, 128), F32)
     lane = lax.broadcasted_iota(jnp.int32, (toks, 128), 1)
     for e in range(experts):
-        weight = jnp.zeros((toks, slots_all), F32)
+        weight = jnp.zeros((slots_all, toks), F32)
         for k in range(len(choice)):
-            part = jnp.sum(jnp.where(pick == k * experts + e, share, 0.0), axis=1, keepdims=True)
+            part = jnp.sum(jnp.where(pick == k * experts + e, share, 0.0), axis=0, keepdims=True)
             weight = weight + choice[k] * part
-        weight_t = (weight * picked).T.astype(BF)
-        gates = gates + jnp.dot(weight_t, (lane == e).astype(BF), preferred_element_type=F32)
+        weight = (weight * picked).astype(BF)
+        gates = gates + jnp.dot(weight, (lane == e).astype(BF), preferred_element_type=F32)
     send[:, :, width:] = gates.astype(BF).reshape(N_OFF, PAD, 128)
 
     def fill_send(i, carry):
@@ -112,9 +113,11 @@
         copy = remote(
             send.at[r], land.at[r], ds_sem.at[r], dr_sem.at[r], (node_at(*OFFS[r]), me_d)
         )
-        copy.start()
         dispatch.append(copy)
+    for r in range(WAVES[0], WAVES[1]):
+        dispatch[r].start()
     land[0] = send[0]
+    sel[...] = picked.T.astype(BF)
 
     def rows_of(k):
         return pl.ds(bounds[k], bounds[k + 1] - bounds[k])
@@ -149,6 +152,32 @@
         return (same & (frm % PAD < CAP)).astype(BF)
 
     arrived = [0]
+    gate_copies = []
+
+    def share_gates(k, pack, got):
+        flat = jnp.dot(pack, got, preferred_element_type=F32).astype(BF)
+        packed = jnp.zeros((PAD, 128), F32)
+        e_at = lax.broadcasted_iota(jnp.int32, (128, 128), 0)
+        l_at = lax.broadcasted_iota(jnp.int32, (128, 128), 1)
+        for t in range(TILES[k]):
+            move = ((e_at < experts) & (l_at == experts * t + e_at)).astype(BF)
+            packed = packed + jnp.dot(
+                flat[t * PAD : (t + 1) * PAD], move, preferred_element_type=F32
+            )
+        gp[k, 0] = packed.astype(BF)
+        copies = []
+        for dx, there in ((0, OWN), (1, LEFT), (3, RIGHT), (2, OPP)):
+            for dc in (0, 1):
+                if (dx, dc) == (0, 0):
+                    continue
+                n = len(copies)
+                copy = remote(
+                    gp.at[k, 0], gp.at[k, 4 * dc + there], gs_sem.at[k, n], gr_sem.at[k, n],
+                    (me_n, dev_at(dx, dc)),
+                )
+                copy.start()
+                copies.append(copy)
+        gate_copies.append(copies)
 
     def deliver(k):
         lo, hi = bounds[k], bounds[k + 1]
@@ -156,7 +185,11 @@
         while arrived[0] < last - 1:
             arrived[0] += 1
             dispatch[arrived[0]].wait_recv()
+        if k + 2 < len(WAVES):
+            for r in range(WAVES[k + 1], WAVES[k + 2]):
+                dispatch[r].start()
         pack = spread(hi - lo, lo, (last - first) * PAD, first * PAD)
+        share_gates(k, pack, land[first:last, :, width:].reshape((last - first) * PAD, 128))
 
         def body(i, carry):
             cols = pl.ds(pl.multiple_of(i * step, step), step)
@@ -164,7 +197,7 @@
             xbuf[OWN, lo:hi, cols] = jnp.dot(pack, got, preferred_element_type=F32).astype(BF)
             return carry
 
-        lax.fori_loop(0, width // step, body, 0)
+        lax.fori_loop(0, width // step, body, 0, unroll=5)
         for j in (0, 1, 4):
             gather[k][j].start()
 
@@ -181,47 +214,21 @@
         gather[k][3].wait_recv()
         gather[k][7].start()
 
-    gate_copies = []
-
-    def share_gates():
-        pack = spread(ROWS, 0, slots_all, 0)
-        got = land[:, :, width:].reshape(slots_all, 128)
-        flat = jnp.dot(pack, got, preferred_element_type=F32).astype(BF)
-        packed = jnp.zeros((PAD, 128), F32)
-        e_at = lax.broadcasted_iota(jnp.int32, (128, 128), 0)
-        l_at = lax.broadcasted_iota(jnp.int32, (128, 128), 1)
-        for t in range(ROWS // PAD):
-            move = ((e_at < experts) & (l_at == experts * t + e_at)).astype(BF)
-            packed = packed + jnp.dot(
-                flat[t * PAD : (t + 1) * PAD], move, preferred_element_type=F32
-            )
-        gp[0] = packed.astype(BF)
-        n = 0
-        for dx, there in ((0, OWN), (1, LEFT), (3, RIGHT), (2, OPP)):
-            for dc in (0, 1):
-                if (dx, dc) == (0, 0):
-                    continue
-                copy = remote(
-                    gp.at[0], gp.at[4 * dc + there], gs_sem.at[n], gr_sem.at[n],
-                    (me_n, dev_at(dx, dc)),
-                )
-                copy.start()
-                gate_copies.append(copy)
-                n += 1
-
     def hidden(k):
         lo, hi = bounds[k], bounds[k + 1]
         m = 8 * (hi - lo)
         for j in (4, 5, 6, 7):
             gather[k][j].wait_recv()
+        for copy in gate_copies[k]:
+            copy.wait_recv()
         contract = (((1,), (1,)), ((), ()))
         columns = []
         for e in range(experts):
             pieces = []
             for s in range(8):
-                for t in range(lo // PAD, hi // PAD):
+                for t in range(TILES[k]):
                     at = experts * t + e
-                    pieces.append(gp[s, :, at : at + 1].astype(F32))
+                    pieces.append(gp[k, s, :, at : at + 1].astype(F32))
             columns.append(jnp.concatenate(pieces, axis=0))
         for e in range(experts):
             rows = xbuf[:, lo:hi, :].reshape(m, width)
@@ -337,7 +344,7 @@
             send[first + own : last, :, cols] = back[own:]
             return carry
 
-        lax.fori_loop(0, width // step, body, 0)
+        lax.fori_loop(0, width // step, body, 0, unroll=5)
         for r in range(first + own, last):
             dz, dy = OFFS[r]
             copy = remote(
@@ -348,39 +355,36 @@
             returns.append(copy)
 
     deliver(0)
+    relay(0)
     deliver(1)
-    relay(0)
+    relay_opp(0)
     deliver(2)
-    relay(1)
-    relay_opp(0)
-    deliver(3)
-    share_gates()
-    relay(2)
-    relay_opp(1)
     for load in loads:
         load.wait()
-    for copy in gate_copies:
-        copy.wait_recv()
     hidden(0)
+    relay(1)
+    deliver(3)
     project(0)
+    relay_opp(1)
+    pass_on(0)
+    relay(2)
+    hidden(1)
     relay(3)
     relay_opp(2)
-    hidden(1)
-    pass_on(0)
     project(1)
+    pass_on(1)
     relay_opp(3)
     pass_home(0)
     hidden(2)
-    pass_on(1)
     project(2)
+    pass_on(2)
     pass_home(1)
     hidden(3)
-    pass_on(2)
     project(3)
     for r in range(1, N_OFF):
         dispatch[r].wait_send()
+    give_back(0)
     pass_on(3)
-    give_back(0)
     pass_home(2)
     give_back(1)
     pass_home(3)
@@ -389,22 +393,32 @@
 
     for r in range(1, N_OFF):
         returns[r].wait_recv()
-
-    def combine(i, carry):
-        cols = pl.ds(pl.multiple_of(i * step, step), step)
-        got = ret[:, :, cols].reshape(slots_all, step)
-        out_ref[:, cols] = jnp.dot(sel[...], got, preferred_element_type=F32).astype(BF)
-        return carry
-
-    lax.fori_loop(0, width // step, combine, 0)
-
-    for copy in gate_copies:
-        copy.wait_send()
+    outs = []
+    parts = 2
+    for p in range(parts):
+
+        def combine(i, carry, p=p):
+            cols = pl.ds(pl.multiple_of(p * (width // parts) + i * step, step), step)
+            got = ret[:, :, cols].reshape(slots_all, step)
+            total[:, cols] = jnp.dot(sel[...], got, preferred_element_type=F32).astype(BF)
+            return carry
+
+        lax.fori_loop(0, width // parts // step, combine, 0, unroll=5)
+        cols = pl.ds(p * (width // parts), width // parts)
+        copy = pltpu.make_async_copy(total.at[:, cols], out_ref.at[:, cols], o_sem.at[p])
+        copy.start()
+        outs.append(copy)
+
+    for copies in gate_copies:
+        for copy in copies:
+            copy.wait_send()
     for k in range(chunks):
         for copy in reduce[k]:
             copy.wait_send()
     for r in range(1, N_OFF):
         returns[r].wait_send()
+    for copy in outs:
+        copy.wait()
 
 
 def shards(tokens, node_ids, expert_pick, gate_share, gate_proj, up_proj, down_proj):
@@ -420,7 +434,7 @@
         kernel,
         out_shape=jax.ShapeDtypeStruct((toks, width), BF),
         in_specs=[vmem] * 4 + [hbm] * 3,
-        out_specs=vmem,
+        out_specs=hbm,
         scratch_shapes=[
             weights,
             weights,
@@ -435,13 +449,15 @@
             pltpu.VMEM((N_OFF, PAD, width + 128), BF),
             pltpu.VMEM((N_OFF, PAD, width), BF),
             pltpu.VMEM((experts, 8 * PAD * max(TILES), units), BF),
-            pltpu.VMEM((8, PAD, 128), BF),
+            pltpu.VMEM((chunks, 8, PAD, 128), BF),
             pltpu.VMEM((toks, N_OFF * PAD), BF),
+            pltpu.VMEM((toks, width), BF),
+            dma((2,)),
             dma((3,)),
             dma((N_OFF,)),
             dma((N_OFF,)),
-            dma((7,)),
-            dma((7,)),
+            dma((chunks, 7)),
+            dma((chunks, 7)),
             dma((chunks, 8)),
             dma((chunks, 8)),
             dma((chunks, 8)),
@@ -452,7 +468,7 @@
         compiler_params=pltpu.CompilerParams(
             collective_id=0, has_side_effects=True, vmem_limit_bytes=67043328
         ),
-    )(tokens, node_ids, expert_pick, gate_share, gate_proj, up_proj, down_proj)
+    )(tokens, node_ids.T, expert_pick.T, gate_share.T, gate_proj, up_proj, down_proj)
 
 
 def solution(mesh):

time: 207 us -> 189 us (0.913)
  Pallas kernels: 201 us -> 187 us
  local copies, waits for them, and re-layouts: 6.1 us -> 1.97 us
    pallas_call x1, Pallas kernels: 201 us -> 187 us  [shards(): pl.pallas_call(kernel, out_shape=jax.ShapeDtypeStruct((toks, width), BF),...]
    unnamed x4 -> x1, local copies, waits for them, and re-layouts: 6.1 us -> 1.97 us
where the time goes in v2:
time: 189 us
  Pallas kernels  187 us (99%)
  local copies, waits for them, and re-layouts  1.97 us (1%)
    pallas_call x1, Pallas kernels, shards(): pl.pallas_call(kernel, out_shape=jax.ShapeDtypeStruct((toks, width), BF),...  187 us

profile of v2, /device:TPU:1, one launch (start us, length us, event | category | flops | bytes accessed | tf_op | source)
XLA Modules:
  0.0 189.3 jit_solution(1782106966009146011)
XLA Ops:
  0.0 187.3 %shard_map.73 = bf16[64,5120]{1,0:T(8,128)(2,1)} custom-call(bf16[64,5120]{1,0:T(8,128)(2,1)} %tok_ref.1, s32[3,64]{1,0:T(4,128)} %bitcast.4, s32[6,64]{1,0:T(8,128)} %bitcast.3, bf16[6,64]{1,0:T(8,128)(2,1)} %bitcast.5, bf16[3,192,5120]{2,1,0:T(8,128)(2,1)} %wg_hbm.1, bf16[3,192,5120]{2,1,0:T(8,128)(2,1)} %wu_hbm.1, bf16[3,192,5120]{2,1,0:T(8,128)(2,1)} %wd_hbm.1), custom_call_target="tpu_custom_call" | custom-call | tf_op jit(solution)/shard_map/pallas_call | solution.py:433
  187.3 2.0 %copy.9 = bf16[64,5120]{1,0:T(8,128)(2,1)} copy(bf16[64,5120]{1,0:T(8,128)(2,1)} %shard_map.73) | data formatting | bytes 1310720

commit v3 on v2

--- a/solution.py
+++ b/solution.py
@@ -15,8 +15,8 @@
 PAD = 16
 OFFS = (
     (0, 0), (0, 1), (1, 0), (3, 3),
-    (2, 2), (1, 2), (2, 1), (0, 2), (2, 0),
-    (3, 2), (2, 3), (3, 1), (1, 3),
+    (2, 2), (1, 2), (2, 1), (3, 2),
+    (2, 3), (0, 2), (2, 0), (3, 1), (1, 3),
     (1, 1), (3, 0), (0, 3),
 )
 N_OFF = len(OFFS)
@@ -384,8 +384,8 @@
     for r in range(1, N_OFF):
         dispatch[r].wait_send()
     give_back(0)
+    pass_home(2)
     pass_on(3)
-    pass_home(2)
     give_back(1)
     pass_home(3)
     give_back(2)

time: 189 us -> 197 us (1.042)
  the two profiles are of different devices: /device:TPU:1 before, /device:TPU:40 now
where the time goes in v3:
time: 197 us; the launch traced here: 196 us
  Pallas kernels  195 us (99%)
  local copies, waits for them, and re-layouts  1.97 us (1%)
    pallas_call x1, Pallas kernels, shards(): pl.pallas_call(kernel, out_shape=jax.ShapeDtypeStruct((toks, width), BF),...  195 us

profile of v3, /device:TPU:40, one launch (start us, length us, event | category | flops | bytes accessed | tf_op | source)
XLA Modules:
  0.0 196.5 jit_solution(17646137023493205454)
XLA Ops:
  0.0 194.5 %shard_map.73 = bf16[64,5120]{1,0:T(8,128)(2,1)} custom-call(bf16[64,5120]{1,0:T(8,128)(2,1)} %tok_ref.1, s32[3,64]{1,0:T(4,128)} %bitcast.4, s32[6,64]{1,0:T(8,128)} %bitcast.3, bf16[6,64]{1,0:T(8,128)(2,1)} %bitcast.5, bf16[3,192,5120]{2,1,0:T(8,128)(2,1)} %wg_hbm.1, bf16[3,192,5120]{2,1,0:T(8,128)(2,1)} %wu_hbm.1, bf16[3,192,5120]{2,1,0:T(8,128)(2,1)} %wd_hbm.1), custom_call_target="tpu_custom_call" | custom-call | tf_op jit(solution)/shard_map/pallas_call | solution.py:433
  194.5 2.0 %copy.9 = bf16[64,5120]{1,0:T(8,128)(2,1)} copy(bf16[64,5120]{1,0:T(8,128)(2,1)} %shard_map.73) | data formatting | bytes 1310720

commit v4 on v3

--- a/solution.py
+++ b/solution.py
@@ -16,7 +16,7 @@
 OFFS = (
     (0, 0), (0, 1), (1, 0), (3, 3),
     (2, 2), (1, 2), (2, 1), (3, 2),
-    (2, 3), (0, 2), (2, 0), (3, 1), (1, 3),
+    (0, 2), (2, 3), (2, 0), (3, 1), (1, 3),
     (1, 1), (3, 0), (0, 3),
 )
 N_OFF = len(OFFS)
@@ -358,35 +358,35 @@
     relay(0)
     deliver(1)
     relay_opp(0)
-    deliver(2)
     for load in loads:
         load.wait()
     hidden(0)
+    project(0)
+    pass_on(0)
     relay(1)
-    deliver(3)
-    project(0)
+    pass_home(0)
+    deliver(2)
     relay_opp(1)
-    pass_on(0)
-    relay(2)
     hidden(1)
-    relay(3)
-    relay_opp(2)
     project(1)
     pass_on(1)
-    relay_opp(3)
-    pass_home(0)
-    hidden(2)
-    project(2)
-    pass_on(2)
-    pass_home(1)
-    hidden(3)
-    project(3)
+    relay(2)
     for r in range(1, N_OFF):
         dispatch[r].wait_send()
     give_back(0)
+    pass_home(1)
+    deliver(3)
+    relay_opp(2)
+    hidden(2)
+    project(2)
+    relay(3)
+    pass_on(2)
+    give_back(1)
+    relay_opp(3)
+    hidden(3)
+    project(3)
     pass_home(2)
     pass_on(3)
-    give_back(1)
     pass_home(3)
     give_back(2)
     give_back(3)

time: 197 us -> 186 us (0.944)
  the two profiles are of different devices: /device:TPU:40 before, /device:TPU:1 now
where the time goes in v4:
time: 186 us
  Pallas kernels  184 us (99%)
  local copies, waits for them, and re-layouts  1.97 us (1%)
    pallas_call x1, Pallas kernels, shards(): pl.pallas_call(kernel, out_shape=jax.ShapeDtypeStruct((toks, width), BF),...  184 us

profile of v4, /device:TPU:1, one launch (start us, length us, event | category | flops | bytes accessed | tf_op | source)
XLA Modules:
  0.0 185.7 jit_solution(13988698489277607728)
XLA Ops:
  0.0 183.8 %shard_map.73 = bf16[64,5120]{1,0:T(8,128)(2,1)} custom-call(bf16[64,5120]{1,0:T(8,128)(2,1)} %tok_ref.1, s32[3,64]{1,0:T(4,128)} %bitcast.4, s32[6,64]{1,0:T(8,128)} %bitcast.3, bf16[6,64]{1,0:T(8,128)(2,1)} %bitcast.5, bf16[3,192,5120]{2,1,0:T(8,128)(2,1)} %wg_hbm.1, bf16[3,192,5120]{2,1,0:T(8,128)(2,1)} %wu_hbm.1, bf16[3,192,5120]{2,1,0:T(8,128)(2,1)} %wd_hbm.1), custom_call_target="tpu_custom_call" | custom-call | tf_op jit(solution)/shard_map/pallas_call | solution.py:433
  183.8 2.0 %copy.9 = bf16[64,5120]{1,0:T(8,128)(2,1)} copy(bf16[64,5120]{1,0:T(8,128)(2,1)} %shard_map.73) | data formatting | bytes 1310720

commit v5 on v4

--- a/solution.py
+++ b/solution.py
@@ -20,7 +20,7 @@
     (1, 1), (3, 0), (0, 3),
 )
 N_OFF = len(OFFS)
-WAVES = (1, 4, 9, N_OFF)
+WAVES = (1, 9, 9, N_OFF)
 ROWS = N_OFF * CAP
 TILES = (3, 4, 4, 2)
 OWN, LEFT, RIGHT, OPP = 0, 1, 2, 3
@@ -364,31 +364,31 @@
     project(0)
     pass_on(0)
     relay(1)
+    deliver(2)
     pass_home(0)
-    deliver(2)
+    deliver(3)
     relay_opp(1)
     hidden(1)
     project(1)
+    relay(2)
     pass_on(1)
-    relay(2)
     for r in range(1, N_OFF):
         dispatch[r].wait_send()
     give_back(0)
-    pass_home(1)
-    deliver(3)
+    relay(3)
     relay_opp(2)
     hidden(2)
+    pass_home(1)
     project(2)
-    relay(3)
     pass_on(2)
-    give_back(1)
     relay_opp(3)
     hidden(3)
     project(3)
+    give_back(1)
     pass_home(2)
     pass_on(3)
+    give_back(2)
     pass_home(3)
-    give_back(2)
     give_back(3)
 
     for r in range(1, N_OFF):

time: 186 us -> 182 us (0.978); the launches traced: 186 us -> 180 us
  Pallas kernels: 184 us -> 178 us
    pallas_call x1, Pallas kernels: 184 us -> 178 us  [shards(): pl.pallas_call(kernel, out_shape=jax.ShapeDtypeStruct((toks, width), BF),...]
where the time goes in v5:
time: 182 us; the launch traced here: 180 us
  Pallas kernels  178 us (98%)
  local copies, waits for them, and re-layouts  1.97 us (1%)
    pallas_call x1, Pallas kernels, shards(): pl.pallas_call(kernel, out_shape=jax.ShapeDtypeStruct((toks, width), BF),...  178 us

profile of v5, /device:TPU:1, one launch (start us, length us, event | category | flops | bytes accessed | tf_op | source)
XLA Modules:
  0.0 179.6 jit_solution(8057122517033616623)
XLA Ops:
  0.0 177.6 %shard_map.73 = bf16[64,5120]{1,0:T(8,128)(2,1)} custom-call(bf16[64,5120]{1,0:T(8,128)(2,1)} %tok_ref.1, s32[3,64]{1,0:T(4,128)} %bitcast.4, s32[6,64]{1,0:T(8,128)} %bitcast.3, bf16[6,64]{1,0:T(8,128)(2,1)} %bitcast.5, bf16[3,192,5120]{2,1,0:T(8,128)(2,1)} %wg_hbm.1, bf16[3,192,5120]{2,1,0:T(8,128)(2,1)} %wu_hbm.1, bf16[3,192,5120]{2,1,0:T(8,128)(2,1)} %wd_hbm.1), custom_call_target="tpu_custom_call" | custom-call | tf_op jit(solution)/shard_map/pallas_call | solution.py:433
  177.6 2.0 %copy.9 = bf16[64,5120]{1,0:T(8,128)(2,1)} copy(bf16[64,5120]{1,0:T(8,128)(2,1)} %shard_map.73) | data formatting | bytes 1310720

commit v6 on v5

--- a/solution.py
+++ b/solution.py
@@ -20,7 +20,7 @@
     (1, 1), (3, 0), (0, 3),
 )
 N_OFF = len(OFFS)
-WAVES = (1, 9, 9, N_OFF)
+WAVES = (1, 4, 9, N_OFF)
 ROWS = N_OFF * CAP
 TILES = (3, 4, 4, 2)
 OWN, LEFT, RIGHT, OPP = 0, 1, 2, 3
@@ -382,13 +382,13 @@
     project(2)
     pass_on(2)
     relay_opp(3)
+    give_back(1)
     hidden(3)
     project(3)
-    give_back(1)
+    pass_on(3)
     pass_home(2)
-    pass_on(3)
+    pass_home(3)
     give_back(2)
-    pass_home(3)
     give_back(3)
 
     for r in range(1, N_OFF):

time: 182 us -> 182 us (level); the launches traced: 180 us -> 182 us
  Pallas kernels: 178 us -> 180 us
    pallas_call x1, Pallas kernels: 178 us -> 180 us  [shards(): pl.pallas_call(kernel, out_shape=jax.ShapeDtypeStruct((toks, width), BF),...]
where the time goes in v6:
time: 182 us
  Pallas kernels  180 us (99%)
  local copies, waits for them, and re-layouts  1.97 us (1%)
    pallas_call x1, Pallas kernels, shards(): pl.pallas_call(kernel, out_shape=jax.ShapeDtypeStruct((toks, width), BF),...  180 us

profile of v6, /device:TPU:1, one launch (start us, length us, event | category | flops | bytes accessed | tf_op | source)
XLA Modules:
  0.0 181.7 jit_solution(6048035539872513)
XLA Ops:
  0.0 179.8 %shard_map.73 = bf16[64,5120]{1,0:T(8,128)(2,1)} custom-call(bf16[64,5120]{1,0:T(8,128)(2,1)} %tok_ref.1, s32[3,64]{1,0:T(4,128)} %bitcast.4, s32[6,64]{1,0:T(8,128)} %bitcast.3, bf16[6,64]{1,0:T(8,128)(2,1)} %bitcast.5, bf16[3,192,5120]{2,1,0:T(8,128)(2,1)} %wg_hbm.1, bf16[3,192,5120]{2,1,0:T(8,128)(2,1)} %wu_hbm.1, bf16[3,192,5120]{2,1,0:T(8,128)(2,1)} %wd_hbm.1), custom_call_target="tpu_custom_call" | custom-call | tf_op jit(solution)/shard_map/pallas_call | solution.py:433
  179.8 2.0 %copy.9 = bf16[64,5120]{1,0:T(8,128)(2,1)} copy(bf16[64,5120]{1,0:T(8,128)(2,1)} %shard_map.73) | data formatting | bytes 1310720
